TPU v7x, 32 devices: a whole 2x2x4 slice. The times are simulated.
32 devices in a mesh: dp: 4 (over z), tensor: 8 (over y, x, core).
Axes of the slice: x: 2, y: 2, z: 4, core: 2. Of those that a mesh axis runs over, the one named last changes fastest.
Arguments:
- activations: bfloat16 [1024, 27648], P('dp', 'tensor'), may hold values from -6 to 6
- left_factor: float32 [216, 216], replicated, may hold values from -2 to 3, as said below
- right_factor: float32 [128, 128], replicated, may hold values from -2 to 3, as said below
- clip_scale: float32 [128, 216], replicated, may hold values from 0.5 to 3
- weight_rows: bfloat16 [27648, 5120], P('tensor'), may hold values from -0.0390625 to 0.0390625
- target: bfloat16 [1024, 5120], P('dp'), may hold values from -6 to 6
Outputs:
- grad_left: float32 [216, 216], replicated
- grad_right: float32 [128, 128], replicated
- grad_input: float32 [1024, 27648], P('dp', 'tensor')
Inputs may be any that keep to these rules, and one draw needn't show every extreme that they name: `left_factor`: the identity plus independent entries of order one over the square root of 216. `right_factor`: the identity plus independent entries of order one over the square root of 128.
All inputs are finite; a program needn't handle non-finite values.
Results may differ from a plain program's by a relative error of at most 0.007.
Values may be sent and summed in bfloat16 or wider, within the bound.
A program may use at most 128 MiB of HBM per device.

v0:
```python
import jax
import jax.numpy as jnp
from jax import lax
from jax.sharding import PartitionSpec as P


def local(activations, left_factor, right_factor, clip_scale, weight_rows, target):
    highest = lax.Precision.HIGHEST
    tok_rows = activations.shape[0]
    width_left = left_factor.shape[0]
    local_right = activations.shape[1] // width_left
    inputs = activations.reshape(tok_rows, local_right, width_left)
    moved = lax.all_to_all(inputs, "tensor", split_axis=0, concat_axis=1, tiled=True)
    mixed = jnp.einsum("tji,ik->tjk", moved.astype(jnp.float32), left_factor, precision=highest)
    rotated = jnp.einsum("jl,tjk->tlk", right_factor, mixed, precision=highest)
    bounded = jnp.tanh(rotated / clip_scale)
    clipped = (clip_scale * bounded).astype(jnp.bfloat16)
    clipped_back = lax.all_to_all(clipped, "tensor", split_axis=1, concat_axis=0, tiled=True)
    partial_out = jnp.dot(
        clipped_back.reshape(tok_rows, -1), weight_rows, preferred_element_type=jnp.float32
    )
    total = lax.psum(partial_out, "tensor")
    out_grad = (total - target.astype(jnp.float32)).astype(jnp.bfloat16)
    clipped_grad = lax.dot_general(
        out_grad, weight_rows, (((1,), (1,)), ((), ())), preferred_element_type=jnp.float32
    )
    clipped_grad = clipped_grad.reshape(tok_rows, local_right, width_left)
    grad_owned = lax.all_to_all(clipped_grad, "tensor", split_axis=0, concat_axis=1, tiled=True)
    rotated_grad = grad_owned * (1.0 - bounded * bounded)
    mixed_grad = jnp.einsum("jl,tlk->tjk", right_factor, rotated_grad, precision=highest)
    right_part = jnp.einsum("tjk,tlk->jl", mixed, rotated_grad, precision=highest)
    grad_back = lax.all_to_all(mixed_grad, "tensor", split_axis=1, concat_axis=0, tiled=True)
    input_grad = jnp.einsum("tjk,ik->tji", grad_back, left_factor, precision=highest).reshape(
        tok_rows, -1
    )
    left_part = jnp.einsum("tji,tjk->ik", inputs.astype(jnp.float32), grad_back, precision=highest)
    left_sum, right_sum = lax.psum((left_part, right_part), ("dp", "tensor"))
    return (left_sum, right_sum, input_grad)


def solution(mesh):
    placed = (P("dp", "tensor"), P(), P(), P(), P("tensor", None), P("dp", None))
    return jax.shard_map(
        local, mesh=mesh, in_specs=placed, out_specs=(P(), P(), P("dp", "tensor")), check_vma=False
    )
```

profile of v0, /device:TPU:8, one launch (start us, length us, event | category | flops | bytes accessed | tf_op | source)
XLA Modules:
  0.0 508.3 jit_solution(451690624203319944)
XLA Ops:
  7.2 0.0 copy-start
  7.2 0.0 all-reduce.4.cloned.1.call-start
  7.2 2.7 copy.31
  9.9 3.0 copy.32
  12.9 30.3 %all_to_all.69 = bf16[256,16,216]{2,1,0:T(8,128)(2,1)S(1)} all-to-all(bf16[256,16,216]{2,1,0:T(8,128)(2,1)} %copy.32), channel_id=1, replica_groups=mesh['dp'=4,'tensor'=8] {'tensor'}, dimensions={0} | all-to-all | bytes 3538944 | tf_op jit(solution)/shard_map/all_to_all | solution.py:13
  43.2 0.3 copy.33
  43.5 0.0 copy-start.2
  43.5 0.0 copy-start.3
  43.5 0.0 copy-done
  43.5 2.1 fusion.6
  45.7 0.0 copy-done.2
  45.7 0.0 copy-done.3
  45.7 0.0 copy-start.1
  45.7 4.7 multiply_convert_fusion
  50.4 0.0 copy-done.1
  50.4 4.5 copy.36
  54.9 30.1 %all_to_all.70 = bf16[32,128,216]{2,0,1:T(8,128)(2,1)S(1)} all-to-all(bf16[32,128,216]{2,0,1:T(8,128)(2,1)} %copy.36), channel_id=1, replica_groups=mesh['dp'=4,'tensor'=8] {'tensor'}, dimensions={1} | all-to-all | bytes 3538944 | tf_op jit(solution)/shard_map/all_to_all | solution.py:18
  85.0 2.6 copy.38
  87.6 5.2 %reshape.21 = bf16[256,3456]{1,0:T(8,128)(2,1)} reshape(bf16[8,32,16,216]{3,2,1,0:T(8,128)(2,1)} %copy.38) | data formatting | bytes 3538944 | tf_op jit(solution)/shard_map/reshape | solution.py:20
  92.8 18.0 %fusion.12 = f32[256,5120]{1,0:T(8,128)} fusion(bf16[256,3456]{1,0:T(8,128)(2,1)} %reshape.21, bf16[3456,5120]{1,0:T(8,128)(2,1)} %param.10), kind=kOutput, calls=%fused_computation.18 | convolution fusion | flops 9059696640 | bytes 42401792 | tf_op jit(solution)/shard_map/dot_general | solution.py:19
  110.8 0.0 all-reduce.4.cloned.1.call-update
  110.8 91.8 %all-reduce.4.cloned.1.call-done = f32[256,5120]{1,0:T(8,128)} async-done(((f32[256,5120]{1,0:T(8,128)}), f32[256,5120]{1,0:T(8,128)}) %all-reduce.4.cloned.1.call-update) | async-done | bytes 5242896 | tf_op jit(solution)/shard_map/psum | solution.py:22
  202.6 19.4 %fusion.1 = f32[256,3456]{0,1:T(8,128)} fusion(bf16[3456,5120]{1,0:T(8,128)(2,1)} %param.10, f32[256,5120]{1,0:T(8,128)} %all-reduce.4.cloned.1.call-done, bf16[256,5120]{1,0:T(8,128)(2,1)} %param.11), kind=kOutput, calls=%fused_computation.5 | convolution fusion | flops 9063628800 | bytes 46792704 | tf_op jit(solution)/shard_map/dot_general | solution.py:24
  222.0 5.3 %copy.40 = f32[256,16,216]{2,1,0:T(8,128)} copy(f32[256,16,216]{0,2,1:T(8,128)} %bitcast.63) | data formatting | bytes 7077888 | tf_op jit(solution)/shard_map/reshape | solution.py:27
  227.3 52.6 %all_to_all.71 = f32[256,16,216]{2,1,0:T(8,128)S(1)} all-to-all(f32[256,16,216]{2,1,0:T(8,128)} %copy.40), channel_id=1, replica_groups=mesh['dp'=4,'tensor'=8] {'tensor'}, dimensions={0} | all-to-all | bytes 7077888 | tf_op jit(solution)/shard_map/all_to_all | solution.py:28
  279.9 2.7 copy.41
  282.6 5.5 %copy.42 = f32[32,128,216]{1,2,0:T(8,128)} copy(f32[32,128,216]{2,1,0:T(8,128)} %bitcast.55) | data formatting | bytes 7077888 | tf_op jit(solution)/shard_map/all_to_all | solution.py:28
  288.1 6.4 %convolution_bitcast_fusion = f32[32,128,216]{1,2,0:T(8,128)} fusion(f32[32,128,216]{1,2,0:T(8,128)} %copy.42, f32[32,128,216]{1,2,0:T(8,128)} %get-tuple-element.15, f32[128,128]{1,0:T(8,128)S(1)} %copy-done.2), kind=kOutput, calls=%fused_computation.6 | convolution fusion | flops 1361608704 | bytes 10682368 | tf_op jit(solution)/shard_map/jl,tlk->tjk/dot_general | solution.py:30
  294.5 5.3 %copy.43 = f32[32,128,216]{2,0,1:T(8,128)} copy(f32[32,128,216]{1,2,0:T(8,128)} %convolution_bitcast_fusion) | data formatting | bytes 7077888 | tf_op jit(solution)/shard_map/jl,tlk->tjk/transpose | solution.py:30
  299.7 4.6 all-to-all-start.3
  304.3 0.3 all-reduce.6.cloned.1.call-start
  304.5 10.7 %fusion.3 = f32[128,128]{1,0:T(8,128)} fusion(f32[32,128,216]{1,2,0:T(8,128)} %copy-done.1, f32[32,128,216]{1,2,0:T(8,128)} %copy.42, f32[32,128,216]{1,2,0:T(8,128)} %get-tuple-element.15), kind=kOutput, calls=%fused_computation.9 | convolution fusion | flops 1361608704 | bytes 10682368 | tf_op jit(solution)/shard_map/tjk,tlk->jl/dot_general | solution.py:31
  315.3 38.1 %all-to-all-done.3 = f32[32,128,216]{2,0,1:T(8,128)} async-done(((f32[32,128,216]{2,0,1:T(8,128)}), f32[32,128,216]{2,0,1:T(8,128)}, u32[]{:S(2)}, u32[]{:S(2)}) %all-to-all-start.3) | async-done | bytes 3538976 | tf_op jit(solution)/shard_map/all_to_all | solution.py:32
  353.4 6.5 %copy.45 = f32[8,32,16,216]{3,2,1,0:T(8,128)} copy(f32[8,32,16,216]{3,1,2,0:T(8,128)} %bitcast.17) | data formatting | bytes 7077888 | tf_op jit(solution)/shard_map/all_to_all | solution.py:32
  359.9 5.1 %copy.46 = f32[256,16,216]{0,2,1:T(8,128)} copy(f32[256,16,216]{2,1,0:T(8,128)} %bitcast.56) | data formatting | bytes 7077888 | tf_op jit(solution)/shard_map/all_to_all | solution.py:32
  365.0 4.6 convolution_bitcast_fusion.1
  369.6 0.0 all-reduce.6.cloned.1.call-update
  369.6 7.1 %fusion.4 = f32[256,16,216]{0,2,1:T(8,128)} fusion(f32[256,16,216]{0,2,1:T(8,128)} %copy.46, f32[216,216]{1,0:T(8,128)S(1)} %copy-done), kind=kOutput, calls=%fused_computation.10 | convolution fusion | flops 2293235712 | bytes 7264512 | tf_op jit(solution)/shard_map/tjk,ik->tji/dot_general | solution.py:33
  376.7 5.2 %copy.49 = f32[256,3456]{1,0:T(8,128)} copy(f32[256,3456]{0,1:T(8,128)} %bitcast.59) | data formatting | bytes 7077888
  381.9 116.3 %all-reduce.6.cloned.1.call-done = (f32[216,216]{0,1:T(8,128)}, f32[128,128]{1,0:T(8,128)}) async-done(((f32[216,216]{0,1:T(8,128)}, f32[128,128]{1,0:T(8,128)}), (f32[216,216]{0,1:T(8,128)}, f32[128,128]{1,0:T(8,128)})) %all-reduce.6.cloned.1.call-update) | async-done | bytes 252176 | tf_op jit(solution)/shard_map/psum | solution.py:37
  498.2 1.7 copy.48
  499.9 1.5 copy.59
Async XLA Ops:
  7.2 36.4 %copy-start = (f32[216,216]{1,0:T(8,128)S(1)}, f32[216,216]{1,0:T(8,128)}, u32[]{:S(2)}) copy-start(f32[216,216]{1,0:T(8,128)} %param.7) | copy-start | bytes 559876
  7.2 195.4 %all-reduce.4.cloned.1.call-start = ((), (), s32[]{:S(2)}) async-start(), calls=%async_computation.4 | async-start | bytes 10485760 | tf_op jit(solution)/shard_map/psum | solution.py:22
  43.5 2.2 copy-start.2
  43.5 2.2 copy-start.3
  45.7 4.7 copy-start.1
  299.7 53.7 %all-to-all-start.3 = ((f32[32,128,216]{2,0,1:T(8,128)}), f32[32,128,216]{2,0,1:T(8,128)}, u32[]{:S(2)}, u32[]{:S(2)}) async-start(f32[32,128,216]{2,0,1:T(8,128)} %copy.43), calls=%async_computation.3 | async-start | bytes 8388608 | tf_op jit(solution)/shard_map/all_to_all | solution.py:32
  304.3 193.9 %all-reduce.6.cloned.1.call-start = ((), (), s32[]{:S(2)}) async-start(), calls=%async_computation.5 | async-start | bytes 573440 | tf_op jit(solution)/shard_map/psum | solution.py:37
Sparse Core Ops, SparseCore 0:
  110.9 91.6 all-reduce.3
  369.7 128.4 all-reduce.5
where the time goes:
time: 510 us; the launch traced here: 508 us
  waiting for transfers between devices  246 us (48%)
  blocking collectives  113 us (22%)
  matrix products  72.9 us (14%)
  local copies, waits for them, and re-layouts  57 us (11%)
  between operations  14.1 us (3%)
    psum x1, waiting for transfers between devices, local(): left_sum, right_sum = lax.psum((left_part, right_part), ('dp', 'tensor'))  116 us
    psum x1, waiting for transfers between devices, local(): total = lax.psum(partial_out, 'tensor')  91.8 us
    all_to_all x1, blocking collectives, local(): lax.all_to_all(clipped_grad, 'tensor', split_axis=0, concat_axis=1, tiled...  52.6 us
    all_to_all x1, waiting for transfers between devices, local(): lax.all_to_all(mixed_grad, 'tensor', split_axis=1, concat_axis=0, tiled=T...  38.1 us
    all_to_all x1, blocking collectives, local(): lax.all_to_all(inputs, 'tensor', split_axis=0, concat_axis=1, tiled=True)  30.3 us
    all_to_all x1, blocking collectives, local(): lax.all_to_all(clipped, 'tensor', split_axis=1, concat_axis=0, tiled=True)  30.1 us
    dot_general x1, matrix products, local(): lax.dot_general(out_grad, weight_rows, (((1,), (1,)), ((), ())), preferre...  19.4 us
    dot_general x1, matrix products, local(): jnp.dot(clipped_back.reshape(tok_rows, -1), weight_rows, preferred_elemen...  18 us
  transfers between devices with their start and end apart: 3, of which 3 were waited for; matrix products, arithmetic and copies ran while one was open for 5% of the time, Pallas kernels for 0%

commit v1 on v0

--- a/solution.py
+++ b/solution.py
@@ -34,7 +34,7 @@
         tok_rows, -1
     )
     left_part = jnp.einsum("tji,tjk->ik", inputs.astype(jnp.float32), grad_back, precision=highest)
-    left_sum, right_sum = lax.psum((left_part, right_part), ("dp", "tensor"))
+    left_sum, right_sum = lax.psum(lax.psum((left_part, right_part), "tensor"), "dp")
     return (left_sum, right_sum, input_grad)
 
 

time: 510 us -> 474 us (0.929)
  waiting for transfers between devices: 246 us -> 209 us
    psum x1 -> x2, waiting for transfers between devices: 116 us -> 78.8 us  [the longest x1 51.9 us: local(): lax.psum((left_part, right_part), 'tensor')]
  transfers between devices with their start and end apart: 3 -> 4, of which waited for: 3 -> 4; matrix products, arithmetic and copies ran while one was open for 5% -> 5% of each run, Pallas kernels for 0% -> 0%
where the time goes in v1:
time: 474 us; the launch traced here: 471 us
  waiting for transfers between devices  209 us (44%)
  blocking collectives  113 us (24%)
  matrix products  73 us (15%)
  local copies, waits for them, and re-layouts  57.1 us (12%)
  between operations  13.8 us (3%)
  starting transfers between devices  5.15 us (1%)
    psum x1, waiting for transfers between devices, local(): total = lax.psum(partial_out, 'tensor')  91.8 us
    all_to_all x1, blocking collectives, local(): lax.all_to_all(clipped_grad, 'tensor', split_axis=0, concat_axis=1, tiled...  52.6 us
    psum x1, waiting for transfers between devices, local(): lax.psum((left_part, right_part), 'tensor')  51.9 us
    all_to_all x1, waiting for transfers between devices, local(): lax.all_to_all(mixed_grad, 'tensor', split_axis=1, concat_axis=0, tiled=T...  38.1 us
    all_to_all x1, blocking collectives, local(): lax.all_to_all(inputs, 'tensor', split_axis=0, concat_axis=1, tiled=True)  30.3 us
    all_to_all x1, blocking collectives, local(): lax.all_to_all(clipped, 'tensor', split_axis=1, concat_axis=0, tiled=True)  30.1 us
    psum x1, waiting for transfers between devices, local(): lax.psum(lax.psum((left_part, right_part), 'tensor'), 'dp')  27 us
    dot_general x1, matrix products, local(): lax.dot_general(out_grad, weight_rows, (((1,), (1,)), ((), ())), preferre...  19.4 us
  transfers between devices with their start and end apart: 4, of which 4 were waited for; matrix products, arithmetic and copies ran while one was open for 5% of the time, Pallas kernels for 0%

profile of v1, /device:TPU:8, one launch (start us, length us, event | category | flops | bytes accessed | tf_op | source)
XLA Modules:
  0.0 470.8 jit_solution(11756191320600356570)
XLA Ops:
  7.2 0.0 copy-start
  7.2 0.0 all-reduce.6.cloned.1.call-start
  7.2 2.7 copy.31
  9.9 3.0 copy.32
  12.9 30.3 %all_to_all.69 = bf16[256,16,216]{2,1,0:T(8,128)(2,1)S(1)} all-to-all(bf16[256,16,216]{2,1,0:T(8,128)(2,1)} %copy.32), channel_id=1, replica_groups=mesh['dp'=4,'tensor'=8] {'tensor'}, dimensions={0} | all-to-all | bytes 3538944 | tf_op jit(solution)/shard_map/all_to_all | solution.py:13
  43.2 0.3 copy.33
  43.5 0.0 copy-start.2
  43.5 0.0 copy-start.3
  43.5 0.0 copy-done
  43.5 2.1 fusion.6
  45.7 0.0 copy-done.2
  45.7 0.0 copy-done.3
  45.7 0.0 copy-start.1
  45.7 4.7 multiply_convert_fusion
  50.4 0.0 copy-done.1
  50.4 4.5 copy.36
  54.9 30.1 %all_to_all.70 = bf16[32,128,216]{2,0,1:T(8,128)(2,1)S(1)} all-to-all(bf16[32,128,216]{2,0,1:T(8,128)(2,1)} %copy.36), channel_id=1, replica_groups=mesh['dp'=4,'tensor'=8] {'tensor'}, dimensions={1} | all-to-all | bytes 3538944 | tf_op jit(solution)/shard_map/all_to_all | solution.py:18
  85.0 2.6 copy.38
  87.6 5.2 %reshape.21 = bf16[256,3456]{1,0:T(8,128)(2,1)} reshape(bf16[8,32,16,216]{3,2,1,0:T(8,128)(2,1)} %copy.38) | data formatting | bytes 3538944 | tf_op jit(solution)/shard_map/reshape | solution.py:20
  92.8 18.0 %fusion.12 = f32[256,5120]{1,0:T(8,128)} fusion(bf16[256,3456]{1,0:T(8,128)(2,1)} %reshape.21, bf16[3456,5120]{1,0:T(8,128)(2,1)} %param.10), kind=kOutput, calls=%fused_computation.18 | convolution fusion | flops 9059696640 | bytes 42401792 | tf_op jit(solution)/shard_map/dot_general | solution.py:19
  110.8 0.0 all-reduce.6.cloned.1.call-update
  110.8 91.8 %all-reduce.6.cloned.1.call-done = f32[256,5120]{1,0:T(8,128)} async-done(((f32[256,5120]{1,0:T(8,128)}), f32[256,5120]{1,0:T(8,128)}) %all-reduce.6.cloned.1.call-update) | async-done | bytes 5242896 | tf_op jit(solution)/shard_map/psum | solution.py:22
  202.6 19.4 %fusion.1 = f32[256,3456]{0,1:T(8,128)} fusion(bf16[3456,5120]{1,0:T(8,128)(2,1)} %param.10, f32[256,5120]{1,0:T(8,128)} %all-reduce.6.cloned.1.call-done, bf16[256,5120]{1,0:T(8,128)(2,1)} %param.11), kind=kOutput, calls=%fused_computation.5 | convolution fusion | flops 9063628800 | bytes 46792704 | tf_op jit(solution)/shard_map/dot_general | solution.py:24
  222.0 5.3 %copy.40 = f32[256,16,216]{2,1,0:T(8,128)} copy(f32[256,16,216]{0,2,1:T(8,128)} %bitcast.63) | data formatting | bytes 7077888 | tf_op jit(solution)/shard_map/reshape | solution.py:27
  227.3 52.6 %all_to_all.71 = f32[256,16,216]{2,1,0:T(8,128)S(1)} all-to-all(f32[256,16,216]{2,1,0:T(8,128)} %copy.40), channel_id=1, replica_groups=mesh['dp'=4,'tensor'=8] {'tensor'}, dimensions={0} | all-to-all | bytes 7077888 | tf_op jit(solution)/shard_map/all_to_all | solution.py:28
  279.9 2.7 copy.41
  282.7 5.5 %copy.42 = f32[32,128,216]{1,2,0:T(8,128)} copy(f32[32,128,216]{2,1,0:T(8,128)} %bitcast.55) | data formatting | bytes 7077888 | tf_op jit(solution)/shard_map/all_to_all | solution.py:28
  288.1 6.4 %convolution_bitcast_fusion = f32[32,128,216]{1,2,0:T(8,128)} fusion(f32[32,128,216]{1,2,0:T(8,128)} %copy.42, f32[32,128,216]{1,2,0:T(8,128)} %get-tuple-element.17, f32[128,128]{1,0:T(8,128)S(1)} %copy-done.2), kind=kOutput, calls=%fused_computation.6 | convolution fusion | flops 1361608704 | bytes 10682368 | tf_op jit(solution)/shard_map/jl,tlk->tjk/dot_general | solution.py:30
  294.5 5.2 %copy.43 = f32[32,128,216]{2,0,1:T(8,128)} copy(f32[32,128,216]{1,2,0:T(8,128)} %convolution_bitcast_fusion) | data formatting | bytes 7077888 | tf_op jit(solution)/shard_map/jl,tlk->tjk/transpose | solution.py:30
  299.8 4.5 all-to-all-start.3
  304.3 0.3 all-reduce.8.cloned.1.call-start
  304.6 10.7 %fusion.3 = f32[128,128]{1,0:T(8,128)} fusion(f32[32,128,216]{1,2,0:T(8,128)} %copy-done.1, f32[32,128,216]{1,2,0:T(8,128)} %copy.42, f32[32,128,216]{1,2,0:T(8,128)} %get-tuple-element.17), kind=kOutput, calls=%fused_computation.9 | convolution fusion | flops 1361608704 | bytes 10682368 | tf_op jit(solution)/shard_map/tjk,tlk->jl/dot_general | solution.py:31
  315.3 38.1 %all-to-all-done.3 = f32[32,128,216]{2,0,1:T(8,128)} async-done(((f32[32,128,216]{2,0,1:T(8,128)}), f32[32,128,216]{2,0,1:T(8,128)}, u32[]{:S(2)}, u32[]{:S(2)}) %all-to-all-start.3) | async-done | bytes 3538976 | tf_op jit(solution)/shard_map/all_to_all | solution.py:32
  353.4 6.6 %copy.45 = f32[8,32,16,216]{3,2,1,0:T(8,128)} copy(f32[8,32,16,216]{3,1,2,0:T(8,128)} %bitcast.17) | data formatting | bytes 7077888 | tf_op jit(solution)/shard_map/all_to_all | solution.py:32
  360.0 5.1 %copy.46 = f32[256,16,216]{0,2,1:T(8,128)} copy(f32[256,16,216]{2,1,0:T(8,128)} %bitcast.56) | data formatting | bytes 7077888 | tf_op jit(solution)/shard_map/all_to_all | solution.py:32
  365.1 4.6 convolution_bitcast_fusion.1
  369.6 0.0 all-reduce.8.cloned.1.call-update
  369.7 0.3 all-reduce.10.cloned.1.call-start
  370.0 51.9 %all-reduce.8.cloned.1.call-done = (f32[216,216]{0,1:T(8,128)}, f32[128,128]{1,0:T(8,128)}) async-done(((f32[216,216]{0,1:T(8,128)}, f32[128,128]{1,0:T(8,128)}), (f32[216,216]{0,1:T(8,128)}, f32[128,128]{1,0:T(8,128)})) %all-reduce.8.cloned.1.call-update) | async-done | bytes 252176 | tf_op jit(solution)/shard_map/psum | solution.py:37
  421.8 0.0 all-reduce.10.cloned.1.call-update
  421.9 7.1 %fusion.4 = f32[256,16,216]{0,2,1:T(8,128)} fusion(f32[256,16,216]{0,2,1:T(8,128)} %copy.46, f32[216,216]{1,0:T(8,128)S(1)} %copy-done), kind=kOutput, calls=%fused_computation.10 | convolution fusion | flops 2293235712 | bytes 7264512 | tf_op jit(solution)/shard_map/tjk,ik->tji/dot_general | solution.py:33
  429.0 5.2 %copy.49 = f32[256,3456]{1,0:T(8,128)} copy(f32[256,3456]{0,1:T(8,128)} %bitcast.59) | data formatting | bytes 7077888
  434.1 27.0 %all-reduce.10.cloned.1.call-done = (f32[216,216]{0,1:T(8,128)}, f32[128,128]{1,0:T(8,128)}) async-done(((f32[216,216]{0,1:T(8,128)}, f32[128,128]{1,0:T(8,128)}), (f32[216,216]{0,1:T(8,128)}, f32[128,128]{1,0:T(8,128)})) %all-reduce.10.cloned.1.call-update) | async-done | bytes 252176 | tf_op jit(solution)/shard_map/psum | solution.py:37
  461.1 1.7 copy.48
  462.8 1.5 copy.61
Async XLA Ops:
  7.2 36.4 %copy-start = (f32[216,216]{1,0:T(8,128)S(1)}, f32[216,216]{1,0:T(8,128)}, u32[]{:S(2)}) copy-start(f32[216,216]{1,0:T(8,128)} %param.7) | copy-start | bytes 559876
  7.2 195.4 %all-reduce.6.cloned.1.call-start = ((), (), s32[]{:S(2)}) async-start(), calls=%async_computation.4 | async-start | bytes 10485760 | tf_op jit(solution)/shard_map/psum | solution.py:22
  43.5 2.2 copy-start.2
  43.5 2.2 copy-start.3
  45.7 4.7 copy-start.1
  299.8 53.6 %all-to-all-start.3 = ((f32[32,128,216]{2,0,1:T(8,128)}), f32[32,128,216]{2,0,1:T(8,128)}, u32[]{:S(2)}, u32[]{:S(2)}) async-start(f32[32,128,216]{2,0,1:T(8,128)} %copy.43), calls=%async_computation.3 | async-start | bytes 8388608 | tf_op jit(solution)/shard_map/all_to_all | solution.py:32
  304.3 117.5 %all-reduce.8.cloned.1.call-start = ((), (), s32[]{:S(2)}) async-start(), calls=%async_computation.5 | async-start | bytes 573440 | tf_op jit(solution)/shard_map/psum | solution.py:37
  369.7 91.4 %all-reduce.10.cloned.1.call-start = ((), (), s32[]{:S(2)}) async-start(), calls=%async_computation.6 | async-start | bytes 573440 | tf_op jit(solution)/shard_map/psum | solution.py:37
Sparse Core Ops, SparseCore 0:
  110.9 91.6 all-reduce.5
  369.8 52.0 all-reduce.7
  424.3 36.7 all-reduce.9
